TPU v7x, 32 devices: a whole 2x2x4 slice. The times are simulated.
32 devices in a mesh: groups: 2 (over y), cells: 8 (over z, x), side: 2 (over core).
Axes of the slice: x: 2, y: 2, z: 4, core: 2. Of those that a mesh axis runs over, the one named last changes fastest.
Arguments:
- datasets: float32 [2, 2000, 8192], P('side', None, ('groups', 'cells')), parts along dimension 2, may hold values from -6 to 6
- sketch: float32 [64, 8192], P(None, ('groups', 'cells')), parts along dimension 1, may hold values from -6 to 6
Outputs:
- factors: float32 [2, 64, 8192], P('side', None, ('groups', 'cells')), parts along dimension 2
There are 2 independent parts, one for each index of `groups`. A program takes and returns all parts, laid end to end along the dimension named above; each array names one. Nothing has to cross between parts.
All inputs are finite; a program needn't handle non-finite values.
Results may differ from a plain program's by a relative error of at most 0.00009.
Values sent between devices are 32-bit elements; how exact they have to be, the bound alone decides.
A program may use at most 64 MiB of HBM per device.

v0:
```python
import functools
import math

import jax
import jax.numpy as jnp
from jax import lax
from jax.experimental import pallas as pl
from jax.experimental.pallas import tpu as pltpu
from jax.sharding import PartitionSpec as P

MESH = pl.DeviceIdType.MESH
F32, BF16 = jnp.float32, jnp.bfloat16
HIGHEST = lax.Precision.HIGHEST
NT = (((1,), (1,)), ((), ()))
NN = (((1,), (0,)), ((), ()))


def each(count, body):
    if count <= 8:
        for index in range(count):
            body(index)
    else:
        lax.fori_loop(0, count, lambda index, carry: (body(index), carry)[1], 0)


def flipped(cell, bits, count):
    bit = 1
    while bit < count:
        own = lax.rem(cell // bit, 2)
        cell = cell + (bits // bit % 2) * (bit - 2 * bit * own)
        bit *= 2
    return cell


def halves(value):
    high = value.astype(BF16)
    low = (value - high.astype(F32)).astype(BF16)
    return high, low


def stacked(value):
    return jnp.concatenate(halves(value), axis=0)


def dot3(small, high, low, dims):
    rows = small.shape[0] // 2
    both = lax.dot_general(small, high, dims, preferred_element_type=F32)
    rest = lax.dot_general(small[:rows], low, dims, preferred_element_type=F32)
    return both[:rows] + (both[rows:] + rest)


def inverse_factor(gram):
    k = gram.shape[0]
    row_ids = lax.broadcasted_iota(jnp.int32, gram.shape, 0)
    lanes = lax.broadcasted_iota(jnp.int32, gram.shape, 1)
    start = jnp.where(lanes < k, (lanes == row_ids).astype(F32), gram)
    step = 8
    blocks = [start[i : i + step] for i in range(0, k, step)]
    ids = lax.broadcasted_iota(jnp.int32, (step, 1), 0)
    for j in range(k):
        b, r = divmod(j, step)
        row = blocks[b][r : r + 1]
        scaled = row / row[:, k + j : k + j + 1]
        for i in range(b, k // step):
            column = blocks[i][:, k + j : k + j + 1]
            if i == b:
                column = jnp.where(ids > r, column, 0.0)
            blocks[i] = blocks[i] - column * scaled
    full = jnp.concatenate(blocks, axis=0)
    pivots = jnp.sum(jnp.where(lanes - k == row_ids, full, 0.0), axis=1, keepdims=True)
    return full / jnp.sqrt(pivots)


def kernel(
    n, owners, chunk, data, sketch, out, stage, drawn, high, low, small, parts, inbox, gathered, acc, grams, total, inverse,
    passing, load_sem, drawn_sem, pass_send, pass_recv, part_send, part_recv, gather_send, gather_recv, gram_send, gram_recv, inv_send, inv_recv,
):
    me, side = lax.axis_index("cells"), lax.axis_index("side")
    genes, width = data.shape[1:]
    k = sketch.shape[0]
    is_x, is_y = side == 0, side == 1
    barrier = pltpu.get_barrier_semaphore()

    def device(cell, which):
        return {"cells": cell, "side": which}

    def greet(s):
        cell = lax.rem(me + s + 1, n)
        pl.semaphore_signal(barrier, inc=1, device_id=device(cell, 1 - side), device_id_type=MESH)

        @pl.when(cell != me)
        def _():
            pl.semaphore_signal(barrier, inc=1, device_id=device(cell, side), device_id_type=MESH)

    relayed = owners == n == 8
    far, far_across = n // 2, n // 2 + 1

    def cell_at(s):
        return flipped(me, s, n) if relayed else lax.rem(me + s, n)

    relay_sums, relay_gathers = relayed, relayed
    part_order = sum_order = gather_order = collect_order = None
    if relayed:
        part_order = ((5, 6, 7, 2, 3, 1, 0, 4), (5, 2, 3, 6, 7, 1, 0, 4)) if relay_sums else (2, 3, 4, 5, 6, 7, 1, 0)
        sum_order = (0, 1, 2, 3, 6, 7, 4) if relay_sums else (0, 1, 2, 3, 4, 5, 6, 7)
        gather_order = ((4, 6, 7, 2, 3, 1), (4, 2, 3, 6, 7, 1)) if relay_gathers else (2, 3, 4, 5, 6, 7, 1)
        collect_order = (0, 1, 4, 2, 3, 6, 7, 5) if relay_gathers else (0, 1, 2, 3, 4, 5, 6, 7)

    def through(order, count, body, start=0):
        if order is None:
            each(count - start, lambda s: body(s + start))
        elif isinstance(order[0], tuple):
            inner = (me >= 2) & (me < 6)
            for test, own_order in zip((inner, jnp.logical_not(inner)), order):

                @pl.when(test)
                def _():
                    through(own_order, count, body, start)
        else:
            for s in order:
                body(s)

    def chunk_at(s):
        return cell_at(s) if relayed else lax.rem(me + 1 + s, owners)

    def start_of(c):
        return pl.multiple_of(jnp.minimum(c * chunk, genes - chunk), 8)

    def load(c):
        return pltpu.make_async_copy(data.at[0, pl.ds(start_of(c), chunk)], stage.at[c], load_sem.at[c])

    draw = pltpu.make_async_copy(sketch, drawn, drawn_sem)
    draw.start()
    through(part_order, owners, lambda s: load(chunk_at(s)).start())
    each(n, greet)

    def prepare(c):
        load(c).wait()
        rows = lax.broadcasted_iota(jnp.int32, (chunk, width), 0)
        value = jnp.where(rows >= c * chunk - start_of(c), stage[c], 0.0)
        high[c], low[c] = halves(value)

    def part_copy(c):
        return pltpu.make_async_remote_copy(
            src_ref=parts.at[c], dst_ref=inbox.at[me], send_sem=part_send.at[c], recv_sem=part_recv.at[me],
            device_id=device(c, 1 - side), device_id_type=MESH,
        )

    def part_arrival(i):
        return pltpu.make_async_remote_copy(
            src_ref=parts.at[0], dst_ref=inbox.at[i], send_sem=part_send.at[0], recv_sem=part_recv.at[i],
            device_id=device(i, 1 - side), device_id_type=MESH,
        )

    def gather_copy(cell, slot, which):
        return pltpu.make_async_remote_copy(
            src_ref=gathered.at[slot], dst_ref=gathered.at[slot], send_sem=gather_send.at[which],
            recv_sem=gather_recv.at[slot], device_id=device(cell, side), device_id_type=MESH,
        )

    def gram_copy(cell, slot, which):
        return pltpu.make_async_remote_copy(
            src_ref=grams.at[slot], dst_ref=grams.at[slot], send_sem=gram_send.at[which],
            recv_sem=gram_recv.at[slot], device_id=device(cell, side), device_id_type=MESH,
        )

    inverse_copy = pltpu.make_async_remote_copy(
        src_ref=inverse, dst_ref=inverse, send_sem=inv_send, recv_sem=inv_recv,
        device_id=device(me, 1 - side), device_id_type=MESH,
    )

    def work_out(s):
        c = chunk_at(s)
        parts[c] = dot3(small[...], high[c], low[c], NT)

    relay_part = pltpu.make_async_remote_copy(
        src_ref=parts.at[cell_at(far_across)], dst_ref=passing, send_sem=pass_send, recv_sem=pass_recv,
        device_id=device(cell_at(1), side), device_id_type=MESH,
    )

    def send(s):
        if relay_sums and s == far_across:
            relay_part.start()
            return
        if relay_sums and s == far:
            relay_part.wait_recv()
            parts[chunk_at(s)] += passing[...]
        part_copy(chunk_at(s)).start()

    def scatter(s):
        work_out(s)
        send(s)

    def prepare_and_work_out(s):
        prepare(chunk_at(s))
        work_out(s)

    draw.wait()

    @pl.when(is_x)
    def _():
        through(part_order, owners, lambda s: prepare(chunk_at(s)))

    @pl.when(is_y)
    def _():
        small[...] = stacked(drawn[...])
        through(part_order, owners, prepare_and_work_out)

    pl.semaphore_wait(barrier, 2 * n - 1)

    @pl.when(is_y)
    def _():
        through(part_order, owners, send)

    @pl.when(me < owners)
    def _():
        def add(s):
            i = cell_at(s)
            part_arrival(i).wait_recv()
            if isinstance(s, int) and s == 0:
                gathered[me] = inbox[i]
            else:
                gathered[me] += inbox[i]

        if relayed:
            through(sum_order, n, add)
        else:
            add(0)
            each(n - 1, lambda s: add(s + 1))
        through(gather_order, n, lambda s: gather_copy(cell_at(s), me, s).start(), 1)

    acc[...] = jnp.zeros_like(acc)

    relay_gather = gather_copy(cell_at(1), cell_at(far), 0) if relay_gathers else None

    def collect(s):
        c = cell_at(s) if relayed else lax.rem(lax.rem(me, owners) - s + owners, owners)

        @pl.when(c != me)
        def _():
            gather_copy(me, c, 0).wait_recv()

        if relay_gathers and s == far:
            relay_gather.start()
        acc[...] += dot3(stacked(gathered[c]), high[c], low[c], NN)

    through(collect_order, owners, collect)

    @pl.when(is_x)
    def _():
        range_rows = acc[...]
        small[...] = stacked(range_rows)
        twice = lax.dot_general(
            range_rows, jnp.concatenate([range_rows, range_rows], axis=0), NT,
            precision=HIGHEST, preferred_element_type=F32,
        )
        left = lax.broadcasted_iota(jnp.int32, grams.shape[1:], 1) < k
        grams[me] = jnp.where(left, twice[: k // 2], twice[k // 2 :])
        each(n - 1, lambda s: gram_copy(lax.rem(me + 1 + s, n), me, s).start())
        through(part_order, owners, scatter)

        def arrive(s):
            gram_copy(me, lax.rem(me - 1 - s + n, n), 0).wait_recv()

        each(n - 1, arrive)
        total[...] = grams[0]

        def add(i):
            total[...] += grams[i + 1]

        each(n - 1, add)
        bottom = total[...]
        gram = jnp.concatenate([pltpu.roll(bottom, k, axis=1), bottom], axis=0)
        inverse[...] = inverse_factor(gram)
        inverse_copy.start()

    @pl.when(is_y)
    def _():
        inverse_copy.wait_recv()

    scale = math.sqrt(width * n)
    factor = jnp.where(is_x, scale, 1.0 / scale).astype(F32)
    out[0] = factor * dot3(stacked(inverse[:, :k]), *halves(acc[...]), NN)

    through(part_order, owners, lambda s: (relay_part if relay_sums and s == far_across else part_copy(chunk_at(s))).wait_send())

    @pl.when(me < owners)
    def _():
        through(gather_order, n, lambda s: gather_copy(cell_at(s), me, s).wait_send(), 1)

    if relay_gathers:
        relay_gather.wait_send()

    @pl.when(is_x)
    def _():
        each(n - 1, lambda s: gram_copy(lax.rem(me + 1 + s, n), me, s).wait_send())
        inverse_copy.wait_send()


def solution(mesh):
    n = mesh.shape["cells"]

    def per_device(datasets, sketch):
        genes, width = datasets.shape[1:]
        k = sketch.shape[0]
        chunk = 128 * -(-genes // (128 * n))
        owners = -(-genes // chunk)
        dma = pltpu.SemaphoreType.DMA
        return pl.pallas_call(
            functools.partial(kernel, n, owners, chunk),
            out_shape=jax.ShapeDtypeStruct((1, k, width), F32),
            in_specs=[pl.BlockSpec(memory_space=pl.ANY)] * 2,
            out_specs=pl.BlockSpec(memory_space=pltpu.VMEM),
            scratch_shapes=[
                pltpu.VMEM((owners, chunk, width), F32),
                pltpu.VMEM((k, width), F32),
                pltpu.VMEM((owners, chunk, width), BF16),
                pltpu.VMEM((owners, chunk, width), BF16),
                pltpu.VMEM((2 * k, width), BF16),
                pltpu.VMEM((owners, k, chunk), F32),
                pltpu.VMEM((n, k, chunk), F32),
                pltpu.VMEM((owners, k, chunk), F32),
                pltpu.VMEM((k, width), F32),
                pltpu.VMEM((n, k // 2, 2 * k), F32),
                pltpu.VMEM((k // 2, 2 * k), F32),
                pltpu.VMEM((k, 2 * k), F32),
                pltpu.VMEM((k, chunk), F32),
                dma((owners,)), dma, dma, dma,
                dma((owners,)), dma((n,)),
                dma((n,)), dma((owners,)),
                dma((n,)), dma((n,)),
                dma, dma,
            ],
            compiler_params=pltpu.CompilerParams(collective_id=0, has_side_effects=True),
            name="power_pass",
        )(datasets, sketch)

    spec = P("side", None, ("groups", "cells"))
    return jax.shard_map(
        per_device, mesh=mesh, in_specs=(spec, P(None, ("groups", "cells"))), out_specs=spec, check_vma=False
    )
```

profile of v0, /device:TPU:1, one launch (start us, length us, event | category | flops | bytes accessed | tf_op | source)
XLA Modules:
  0.0 39.8 jit_solution(8029252812388510280)
XLA Ops:
  0.0 38.3 %power_pass.1 = f32[1,64,512]{2,1,0:T(8,128)} custom-call(f32[1,2000,512]{2,1,0:T(8,128)} %data.1, f32[64,512]{1,0:T(8,128)} %sketch.1), custom_call_target="tpu_custom_call" | custom-call | tf_op jit(solution)/shard_map/power_pass/pallas_call | solution.py:309
  38.3 1.6 %copy.4 = f32[1,64,512]{2,1,0:T(8,128)} copy(f32[1,64,512]{2,1,0:T(8,128)} %power_pass.1) | data formatting | bytes 262144
where the time goes:
time: 40 us; the launch traced here: 39.8 us
  Pallas kernels  38.3 us (96%)
  local copies, waits for them, and re-layouts  1.57 us (4%)
    pallas_call x1, Pallas kernels, per_device(): pl.pallas_call(functools.partial(kernel, n, owners, chunk), out_shape=jax...  38.3 us
    unnamed x1, local copies, waits for them, and re-layouts  1.57 us

commit v1 on v0

v1 whole, which is shorter than its diff:
```python
import functools
import math

import jax
import jax.numpy as jnp
from jax import lax
from jax.experimental import pallas as pl
from jax.experimental.pallas import tpu as pltpu
from jax.sharding import PartitionSpec as P

MESH = pl.DeviceIdType.MESH
F32, BF16 = jnp.float32, jnp.bfloat16
HIGHEST = lax.Precision.HIGHEST
NT = (((1,), (1,)), ((), ()))
NN = (((1,), (0,)), ((), ()))


def each(count, body):
    if count <= 8:
        for index in range(count):
            body(index)
    else:
        lax.fori_loop(0, count, lambda index, carry: (body(index), carry)[1], 0)


def flipped(cell, bits, count):
    bit = 1
    while bit < count:
        own = lax.rem(cell // bit, 2)
        cell = cell + (bits // bit % 2) * (bit - 2 * bit * own)
        bit *= 2
    return cell


def halves(value):
    high = value.astype(BF16)
    low = (value - high.astype(F32)).astype(BF16)
    return high, low


def stacked(value):
    return jnp.concatenate(halves(value), axis=0)


def dot3(small, high, low, dims):
    rows = small.shape[0] // 2
    both = lax.dot_general(small, high, dims, preferred_element_type=F32)
    rest = lax.dot_general(small[:rows], low, dims, preferred_element_type=F32)
    return both[:rows] + (both[rows:] + rest)


def inverse_factor(gram):
    k = gram.shape[0]
    row_ids = lax.broadcasted_iota(jnp.int32, gram.shape, 0)
    lanes = lax.broadcasted_iota(jnp.int32, gram.shape, 1)
    start = jnp.where(lanes < k, (lanes == row_ids).astype(F32), gram)
    step = 8
    blocks = [start[i : i + step] for i in range(0, k, step)]
    ids = lax.broadcasted_iota(jnp.int32, (step, gram.shape[1]), 0)

    def spread(block, lane):
        return jnp.broadcast_to(block[:, lane : lane + 1], block.shape)

    for b in range(k // step):
        first = k + step * b
        block = blocks[b]
        pivot_columns = [spread(block, first + r) for r in range(step)]
        reciprocals = []
        for r in range(step):
            reciprocals.append(1.0 / pivot_columns[r][r : r + 1])
            ratio = jnp.where(ids > r, pivot_columns[r], 0.0) * reciprocals[r]
            block = block - ratio * block[r : r + 1]
            for j in range(r + 1, step):
                pivot_columns[j] = pivot_columns[j] - ratio * pivot_columns[j][r : r + 1]
        for i in range(b + 1, k // step):
            columns = [spread(blocks[i], first + r) for r in range(step)]
            below = blocks[i]
            for r in range(step):
                ratio = columns[r] * reciprocals[r]
                below = below - ratio * block[r : r + 1]
                for j in range(r + 1, step):
                    columns[j] = columns[j] - ratio * pivot_columns[j][r : r + 1]
            blocks[i] = below
        blocks[b] = block
    full = jnp.concatenate(blocks, axis=0)
    pivots = jnp.sum(jnp.where(lanes - k == row_ids, full, 0.0), axis=1, keepdims=True)
    return full / jnp.sqrt(pivots)


def kernel(
    n, owners, chunk, splits, data, sketch, out, stage, drawn, high, low, high_t, low_t, small, parts, inbox, gathered, acc, grams, total, inverse,
    load_sem, drawn_sem, part_send, part_recv, gather_send, gather_recv, gram_send, gram_recv, inv_send, inv_recv,
):
    me, side = lax.axis_index("cells"), lax.axis_index("side")
    genes, width = data.shape[1:]
    k = sketch.shape[0]
    rows = k // splits
    is_x, is_y = side == 0, side == 1
    barrier = pltpu.get_barrier_semaphore()
    paired = owners == n == 8
    first_parts = second_parts = first_gathers = second_gathers = collect_order = None
    if paired:
        first_parts = ((5, 4, 7, 6, 2, 1, 3, 0), (7, 6, 5, 1, 3, 2, 4, 0))
        second_parts = ((5, 4, 7, 6, 2, 3, 1, 0), (6, 1, 5, 4, 3, 2, 7, 0))
        first_gathers = ((5, 4, 7, 6, 3, 2, 1), (7, 6, 5, 4, 3, 2, 1))
        second_gathers = ((5, 4, 7, 6, 3, 2, 1), (7, 6, 5, 4, 3, 2, 1))
        collect_order = (0, 1, 2, 3, 4, 6, 7, 5)

    def device(cell, which):
        return {"cells": cell, "side": which}

    def cell_at(s):
        return flipped(me, s, n) if paired else lax.rem(me + s, n)

    def chunk_at(s):
        return cell_at(s) if paired else lax.rem(me + 1 + s, owners)

    def slot(s):
        return s if paired else chunk_at(s)

    def through(order, count, body, start=0, group=1):
        if order is None:
            each(count - start, lambda s: body((s + start,)))
        elif isinstance(order[0], tuple):
            inner = (me >= 2) & (me < 6)
            for test, own_order in zip((inner, jnp.logical_not(inner)), order):

                @pl.when(test)
                def _():
                    through(own_order, count, body, start, group)
        else:
            for i in range(0, len(order), group):
                body(order[i : i + group])

    def start_of(c):
        return pl.multiple_of(jnp.minimum(c * chunk, genes - chunk), 8)

    def load(s):
        return pltpu.make_async_copy(
            data.at[0, pl.ds(start_of(chunk_at(s)), chunk)], stage.at[slot(s)], load_sem.at[slot(s)]
        )

    def part_copy(h, s):
        there = s if paired else me
        return pltpu.make_async_remote_copy(
            src_ref=parts.at[h, slot(s)], dst_ref=inbox.at[h, there], send_sem=part_send.at[h, slot(s)],
            recv_sem=part_recv.at[h, there], device_id=device(chunk_at(s), 1 - side), device_id_type=MESH,
        )

    def part_arrival(h, s):
        here = s if paired else cell_at(s)
        pltpu.make_async_remote_copy(
            src_ref=parts.at[h, 0], dst_ref=inbox.at[h, here], send_sem=part_send.at[h, 0],
            recv_sem=part_recv.at[h, here], device_id=device(cell_at(s), 1 - side), device_id_type=MESH,
        ).wait_recv()
        return inbox[h, here]

    own = 0 if paired else me

    def gather_copy(h, s):
        there = s if paired else me
        return pltpu.make_async_remote_copy(
            src_ref=gathered.at[h, own], dst_ref=gathered.at[h, there], send_sem=gather_send.at[h, s],
            recv_sem=gather_recv.at[h, there], device_id=device(cell_at(s), side), device_id_type=MESH,
        )

    def gather_arrival(h, here):
        pltpu.make_async_remote_copy(
            src_ref=gathered.at[h, here], dst_ref=gathered.at[h, here], send_sem=gather_send.at[h, 0],
            recv_sem=gather_recv.at[h, here], device_id=device(me, side), device_id_type=MESH,
        ).wait_recv()

    def gram_copy(cell, where, which):
        return pltpu.make_async_remote_copy(
            src_ref=grams.at[where], dst_ref=grams.at[where], send_sem=gram_send.at[which],
            recv_sem=gram_recv.at[where], device_id=device(cell, side), device_id_type=MESH,
        )

    inverse_copy = pltpu.make_async_remote_copy(
        src_ref=inverse, dst_ref=inverse, send_sem=inv_send, recv_sem=inv_recv,
        device_id=device(me, 1 - side), device_id_type=MESH,
    )

    draw = pltpu.make_async_copy(sketch, drawn, drawn_sem)
    draw.start()
    through(first_parts, owners, lambda group: [load(s).start() for s in group])

    @pl.when(is_x)
    def _():
        each(n, lambda s: pl.semaphore_signal(
            barrier, inc=1, device_id=device(lax.rem(me + s, n), 1 - side), device_id_type=MESH
        ))

    def prepare(s):
        value = stage[slot(s)]
        twice = owners * chunk - genes
        if twice:
            c = chunk_at(s)
            ids = lax.broadcasted_iota(jnp.int32, (twice, width), 0)
            first = jnp.where(ids >= c * chunk - start_of(c), value[:twice], 0.0)
            value = jnp.concatenate([first, value[twice:]], axis=0)
        high[slot(s)], low[slot(s)] = halves(value)

    def prepare_all(group):
        for s in group:
            load(s).wait()
        for s in group:
            prepare(s)

    def prepare_and_work_out(group):
        prepare_all(group)
        values = [dot3(small[...], high[slot(s)], low[slot(s)], NT) for s in group]
        for s, value in zip(group, values):
            for h in range(splits):
                parts[h, slot(s)] = value[h * rows : (h + 1) * rows]

    def turn(c):
        high_t[c], low_t[c] = high[c].T, low[c].T

    draw.wait()

    @pl.when(is_x)
    def _():
        through(first_parts, owners, prepare_all)
        each(owners, turn)

    @pl.when(is_y)
    def _():
        small[...] = stacked(drawn[...])
        through(first_parts, owners, prepare_and_work_out, group=4)
        pl.semaphore_wait(barrier, n)
        for h in range(splits):
            through(first_parts, owners, lambda group: [part_copy(h, s).start() for s in group])

    @pl.when(me < owners)
    def _():
        for h in range(splits):

            def add(s):
                gathered[h, own] += part_arrival(h, s)

            gathered[h, own] = part_arrival(h, 0)
            each(n - 1, lambda s: add(s + 1))
            for test, order in ((is_x, first_gathers), (is_y, second_gathers)):

                @pl.when(test)
                def _():
                    through(order, n, lambda group: [gather_copy(h, s).start() for s in group], 1)

    acc[...] = jnp.zeros_like(acc)

    def collect(h, s):
        if paired:
            c = s
            if s:
                gather_arrival(h, s)
        else:
            c = lax.rem(lax.rem(me, owners) - s + owners, owners)

            @pl.when(c != me)
            def _():
                gather_arrival(h, c)

        acc[h] += dot3(stacked(gathered[h, c]), high[c], low[c], NN)

    def scatter(h, group):
        mine = small[2 * rows * h : 2 * rows * (h + 1)]
        values = [dot3(mine, high_t[slot(s)], low_t[slot(s)], NN) for s in group]
        for s, value in zip(group, values):
            parts[h, slot(s)] = value
        for s in group:
            part_copy(h, s).start()

    for h in range(splits):
        through(collect_order, owners, lambda group: [collect(h, s) for s in group])

        @pl.when(is_x)
        def _():
            small[2 * rows * h : 2 * rows * (h + 1)] = stacked(acc[h])
            through(second_parts, owners, lambda group: scatter(h, group), group=4)

    @pl.when(is_x)
    def _():
        range_rows = jnp.concatenate([acc[i] for i in range(splits)], axis=0)
        twice = lax.dot_general(
            range_rows, jnp.concatenate([range_rows, range_rows], axis=0), NT,
            precision=HIGHEST, preferred_element_type=F32,
        )
        left = lax.broadcasted_iota(jnp.int32, grams.shape[1:], 1) < k
        grams[me] = jnp.where(left, twice[: k // 2], twice[k // 2 :])
        each(n - 1, lambda s: gram_copy(lax.rem(me + 1 + s, n), me, s).start())

        def arrive(s):
            gram_copy(me, lax.rem(me - 1 - s + n, n), 0).wait_recv()

        each(n - 1, arrive)
        total[...] = grams[0]

        def add(i):
            total[...] += grams[i + 1]

        each(n - 1, add)
        bottom = total[...]
        gram = jnp.concatenate([pltpu.roll(bottom, k, axis=1), bottom], axis=0)
        inverse[...] = inverse_factor(gram)
        inverse_copy.start()

    @pl.when(is_y)
    def _():
        inverse_copy.wait_recv()

    scale = math.sqrt(width * n)
    factor = jnp.where(is_x, scale, 1.0 / scale).astype(F32)
    full = jnp.concatenate([acc[h] for h in range(splits)], axis=0)
    out[0] = factor * dot3(stacked(inverse[:, :k]), *halves(full), NN)

    for h in range(splits):
        each(owners, lambda s: part_copy(h, s).wait_send())

        @pl.when(me < owners)
        def _():
            each(n - 1, lambda s: gather_copy(h, s + 1).wait_send())

    @pl.when(is_x)
    def _():
        each(n - 1, lambda s: gram_copy(lax.rem(me + 1 + s, n), me, s).wait_send())
        inverse_copy.wait_send()


def solution(mesh):
    n = mesh.shape["cells"]

    def per_device(datasets, sketch):
        genes, width = datasets.shape[1:]
        k = sketch.shape[0]
        chunk = 128 * -(-genes // (128 * n))
        owners = -(-genes // chunk)
        splits = 2 if owners == n == 8 and k % 16 == 0 else 1
        rows = k // splits
        dma = pltpu.SemaphoreType.DMA
        return pl.pallas_call(
            functools.partial(kernel, n, owners, chunk, splits),
            out_shape=jax.ShapeDtypeStruct((1, k, width), F32),
            in_specs=[pl.BlockSpec(memory_space=pl.ANY)] * 2,
            out_specs=pl.BlockSpec(memory_space=pltpu.VMEM),
            scratch_shapes=[
                pltpu.VMEM((owners, chunk, width), F32),
                pltpu.VMEM((k, width), F32),
                pltpu.VMEM((owners, chunk, width), BF16),
                pltpu.VMEM((owners, chunk, width), BF16),
                pltpu.VMEM((owners, width, chunk), BF16),
                pltpu.VMEM((owners, width, chunk), BF16),
                pltpu.VMEM((2 * k, width), BF16),
                pltpu.VMEM((splits, owners, rows, chunk), F32),
                pltpu.VMEM((splits, n, rows, chunk), F32),
                pltpu.VMEM((splits, owners, rows, chunk), F32),
                pltpu.VMEM((splits, rows, width), F32),
                pltpu.VMEM((n, k // 2, 2 * k), F32),
                pltpu.VMEM((k // 2, 2 * k), F32),
                pltpu.VMEM((k, 2 * k), F32),
                dma((owners,)), dma,
                dma((splits, owners)), dma((splits, n)),
                dma((splits, n)), dma((splits, owners)),
                dma((n,)), dma((n,)),
                dma, dma,
            ],
            compiler_params=pltpu.CompilerParams(collective_id=0, has_side_effects=True),
            name="power_pass",
        )(datasets, sketch)

    spec = P("side", None, ("groups", "cells"))
    return jax.shard_map(
        per_device, mesh=mesh, in_specs=(spec, P(None, ("groups", "cells"))), out_specs=spec, check_vma=False
    )
```

time: 40 us -> 37.1 us (0.927)
  Pallas kernels: 38.3 us -> 35.4 us
    pallas_call x1, Pallas kernels: 38.3 us -> 35.4 us  [per_device(): pl.pallas_call(functools.partial(kernel, n, owners, chunk, splits), out_s...]
where the time goes in v1:
time: 37.1 us; the launch traced here: 37 us
  Pallas kernels  35.4 us (95%)
  local copies, waits for them, and re-layouts  1.57 us (4%)
    pallas_call x1, Pallas kernels, per_device(): pl.pallas_call(functools.partial(kernel, n, owners, chunk, splits), out_s...  35.4 us
    unnamed x1, local copies, waits for them, and re-layouts  1.57 us

profile of v1, /device:TPU:1, one launch (start us, length us, event | category | flops | bytes accessed | tf_op | source)
XLA Modules:
  0.0 37.0 jit_solution(13962537870075074459)
XLA Ops:
  0.0 35.4 %power_pass.1 = f32[1,64,512]{2,1,0:T(8,128)} custom-call(f32[1,2000,512]{2,1,0:T(8,128)} %data.1, f32[64,512]{1,0:T(8,128)} %sketch.1), custom_call_target="tpu_custom_call" | custom-call | tf_op jit(solution)/shard_map/power_pass/pallas_call | solution.py:341
  35.4 1.6 %copy.4 = f32[1,64,512]{2,1,0:T(8,128)} copy(f32[1,64,512]{2,1,0:T(8,128)} %power_pass.1) | data formatting | bytes 262144

commit v2 on v1

--- a/solution.py
+++ b/solution.py
@@ -340,7 +340,7 @@
         dma = pltpu.SemaphoreType.DMA
         return pl.pallas_call(
             functools.partial(kernel, n, owners, chunk, splits),
-            out_shape=jax.ShapeDtypeStruct((1, k, width), F32),
+            out_shape=pltpu.VMEM((1, k, width), F32),
             in_specs=[pl.BlockSpec(memory_space=pl.ANY)] * 2,
             out_specs=pl.BlockSpec(memory_space=pltpu.VMEM),
             scratch_shapes=[

time: 37.1 us -> 35.6 us (0.960)
  local copies, waits for them, and re-layouts: 1.57 us -> 0.66 us
  Pallas kernels: 35.4 us -> 34.8 us
    unnamed x1, local copies, waits for them, and re-layouts: 1.57 us -> 0.66 us
    pallas_call x1, Pallas kernels: 35.4 us -> 34.8 us  [per_device(): pl.pallas_call(functools.partial(kernel, n, owners, chunk, splits), out_s...]
where the time goes in v2:
time: 35.6 us; the launch traced here: 35.5 us
  Pallas kernels  34.8 us (98%)
  local copies, waits for them, and re-layouts  0.66 us (2%)
    pallas_call x1, Pallas kernels, per_device(): pl.pallas_call(functools.partial(kernel, n, owners, chunk, splits), out_s...  34.8 us

profile of v2, /device:TPU:1, one launch (start us, length us, event | category | flops | bytes accessed | tf_op | source)
XLA Modules:
  0.0 35.5 jit_solution(17792602358037597748)
XLA Ops:
  0.0 34.8 %power_pass.1 = f32[1,64,512]{2,1,0:T(8,128)S(1)} custom-call(f32[1,2000,512]{2,1,0:T(8,128)} %data.1, f32[64,512]{1,0:T(8,128)} %sketch.1), custom_call_target="tpu_custom_call" | custom-call | tf_op jit(solution)/shard_map/power_pass/pallas_call | solution.py:341
  34.8 0.7 %copy.4 = f32[1,64,512]{2,1,0:T(8,128)} copy(f32[1,64,512]{2,1,0:T(8,128)S(1)} %power_pass.1) | data formatting | bytes 262144

commit v3 on v2

--- a/solution.py
+++ b/solution.py
@@ -89,7 +89,7 @@
 
 def kernel(
     n, owners, chunk, splits, data, sketch, out, stage, drawn, high, low, high_t, low_t, small, parts, inbox, gathered, acc, grams, total, inverse,
-    load_sem, drawn_sem, part_send, part_recv, gather_send, gather_recv, gram_send, gram_recv, inv_send, inv_recv,
+    passing, load_sem, drawn_sem, part_send, part_recv, pass_recv, gather_send, gather_recv, gram_send, gram_recv, inv_send, inv_recv,
 ):
     me, side = lax.axis_index("cells"), lax.axis_index("side")
     genes, width = data.shape[1:]
@@ -98,13 +98,21 @@
     is_x, is_y = side == 0, side == 1
     barrier = pltpu.get_barrier_semaphore()
     paired = owners == n == 8
-    first_parts = second_parts = first_gathers = second_gathers = collect_order = None
+    loads = first_sends = second_parts = first_gathers = second_gathers = first_collect = second_collect = None
+    relayed_parts = relayed_gathers = ()
     if paired:
-        first_parts = ((5, 4, 7, 6, 2, 1, 3, 0), (7, 6, 5, 1, 3, 2, 4, 0))
+        loads = ((5, 4, 7, 6, 2, 1, 3, 0), (7, 6, 5, 1, 3, 2, 4, 0))
+        first_sends = (
+            (5, 4, 7, 6, 2, 1, 3, 0, 13, 12, 15, 14, 10, 9, 11, 8),
+            (7, 6, 5, 1, 3, 2, 4, 0, 15, 14, 13, 9, 11, 10, 12, 8),
+        )
         second_parts = ((5, 4, 7, 6, 2, 3, 1, 0), (6, 1, 5, 4, 3, 2, 7, 0))
         first_gathers = ((5, 4, 7, 6, 3, 2, 1), (7, 6, 5, 4, 3, 2, 1))
         second_gathers = ((5, 4, 7, 6, 3, 2, 1), (7, 6, 5, 4, 3, 2, 1))
-        collect_order = (0, 1, 2, 3, 4, 6, 7, 5)
+        first_collect = (0, 1, 2, 3, 4, 6, 7, 5)
+        second_collect = (0, 1, 2, 3, 4, 6, 7, 5)
+        relayed_parts = ()
+        relayed_gathers = ()
 
     def device(cell, which):
         return {"cells": cell, "side": which}
@@ -155,6 +163,12 @@
         ).wait_recv()
         return inbox[h, here]
 
+    def relay_part(h, s):
+        return pltpu.make_async_remote_copy(
+            src_ref=parts.at[h, s], dst_ref=passing.at[h, s - 1], send_sem=part_send.at[h, s],
+            recv_sem=pass_recv.at[h, s - 1], device_id=device(cell_at(1), side), device_id_type=MESH,
+        )
+
     own = 0 if paired else me
 
     def gather_copy(h, s):
@@ -170,6 +184,12 @@
             recv_sem=gather_recv.at[h, here], device_id=device(me, side), device_id_type=MESH,
         ).wait_recv()
 
+    def relay_gather(h, s):
+        return pltpu.make_async_remote_copy(
+            src_ref=gathered.at[h, s], dst_ref=gathered.at[h, s + 1], send_sem=gather_send.at[h, s + 1],
+            recv_sem=gather_recv.at[h, s + 1], device_id=device(cell_at(1), side), device_id_type=MESH,
+        )
+
     def gram_copy(cell, where, which):
         return pltpu.make_async_remote_copy(
             src_ref=grams.at[where], dst_ref=grams.at[where], send_sem=gram_send.at[which],
@@ -183,13 +203,28 @@
 
     draw = pltpu.make_async_copy(sketch, drawn, drawn_sem)
     draw.start()
-    through(first_parts, owners, lambda group: [load(s).start() for s in group])
+    through(loads, owners, lambda group: [load(s).start() for s in group])
 
     @pl.when(is_x)
     def _():
         each(n, lambda s: pl.semaphore_signal(
             barrier, inc=1, device_id=device(lax.rem(me + s, n), 1 - side), device_id_type=MESH
         ))
+
+    if relayed_parts:
+
+        @pl.when(is_y)
+        def _():
+            pl.semaphore_signal(barrier, inc=1, device_id=device(cell_at(1), side), device_id_type=MESH)
+
+    def send_first(h, s):
+        if s in relayed_parts:
+            relay_part(h, s).start()
+            return
+        if s + 1 in relayed_parts:
+            relay_part(h, s + 1).wait_recv()
+            parts[h, s] += passing[h, s]
+        part_copy(h, s).start()
 
     def prepare(s):
         value = stage[slot(s)]
@@ -221,39 +256,51 @@
 
     @pl.when(is_x)
     def _():
-        through(first_parts, owners, prepare_all)
+        through(loads, owners, prepare_all)
         each(owners, turn)
 
     @pl.when(is_y)
     def _():
         small[...] = stacked(drawn[...])
-        through(first_parts, owners, prepare_and_work_out, group=4)
-        pl.semaphore_wait(barrier, n)
-        for h in range(splits):
-            through(first_parts, owners, lambda group: [part_copy(h, s).start() for s in group])
-
-    @pl.when(me < owners)
-    def _():
+        through(loads, owners, prepare_and_work_out, group=4)
+        pl.semaphore_wait(barrier, n + 1 if relayed_parts else n)
+        if paired:
+            through(first_sends, splits * owners, lambda group: [send_first(*divmod(t, owners)) for t in group])
+        else:
+            each(owners, lambda s: part_copy(0, s).start())
+
+    def total_up(skipped, order):
         for h in range(splits):
 
             def add(s):
                 gathered[h, own] += part_arrival(h, s)
 
             gathered[h, own] = part_arrival(h, 0)
-            each(n - 1, lambda s: add(s + 1))
-            for test, order in ((is_x, first_gathers), (is_y, second_gathers)):
-
-                @pl.when(test)
-                def _():
-                    through(order, n, lambda group: [gather_copy(h, s).start() for s in group], 1)
+            if paired:
+                for s in (1, 2, 3, 6, 7, 4, 5):
+                    if s not in skipped:
+                        add(s)
+            else:
+                each(n - 1, lambda s: add(s + 1))
+            through(order, n, lambda group: [gather_copy(h, s).start() for s in group], 1)
+
+    @pl.when(is_x & (me < owners))
+    def _():
+        total_up(relayed_parts, first_gathers)
+
+    @pl.when(is_y & (me < owners))
+    def _():
+        total_up((), second_gathers)
 
     acc[...] = jnp.zeros_like(acc)
 
-    def collect(h, s):
+    def collect(h, s, relayed):
         if paired:
             c = s
             if s:
                 gather_arrival(h, s)
+            if s + 1 in relayed:
+                relay_gather(h, s).start()
         else:
             c = lax.rem(lax.rem(me, owners) - s + owners, owners)
 
@@ -263,32 +310,57 @@
 
         acc[h] += dot3(stacked(gathered[h, c]), high[c], low[c], NN)
 
-    def scatter(h, group):
-        mine = small[2 * rows * h : 2 * rows * (h + 1)]
-        values = [dot3(mine, high_t[slot(s)], low_t[slot(s)], NN) for s in group]
-        for s, value in zip(group, values):
-            parts[h, slot(s)] = value
-        for s in group:
-            part_copy(h, s).start()
-
-    for h in range(splits):
-        through(collect_order, owners, lambda group: [collect(h, s) for s in group])
-
-        @pl.when(is_x)
-        def _():
-            small[2 * rows * h : 2 * rows * (h + 1)] = stacked(acc[h])
-            through(second_parts, owners, lambda group: scatter(h, group), group=4)
-
-    @pl.when(is_x)
-    def _():
+    lanes = lax.broadcasted_iota(jnp.int32, grams.shape[1:], 1)
+
+    def work_out_gram():
+        if splits == 2:
+            products = lax.dot_general(small[...], small[...], NT, preferred_element_type=F32)
+            pair = [products[2 * rows * h : 2 * rows * h + rows] + products[2 * rows * h + rows : 2 * rows * (h + 1)] for h in range(2)]
+            top, bottom = [value + pltpu.roll(value, 2 * k - rows, axis=1) for value in pair]
+            grams[me] = jnp.where(lax.rem(lanes, k) < rows, top, pltpu.roll(bottom, rows, axis=1))
+            return
         range_rows = jnp.concatenate([acc[i] for i in range(splits)], axis=0)
         twice = lax.dot_general(
             range_rows, jnp.concatenate([range_rows, range_rows], axis=0), NT,
             precision=HIGHEST, preferred_element_type=F32,
         )
-        left = lax.broadcasted_iota(jnp.int32, grams.shape[1:], 1) < k
-        grams[me] = jnp.where(left, twice[: k // 2], twice[k // 2 :])
+        grams[me] = jnp.where(lanes < k, twice[: k // 2], twice[k // 2 :])
+
+    def send_gram():
         each(n - 1, lambda s: gram_copy(lax.rem(me + 1 + s, n), me, s).start())
+
+    def scatter(h, group, with_gram):
+        mine = small[2 * rows * h : 2 * rows * (h + 1)]
+        values = [dot3(mine, high_t[slot(s)], low_t[slot(s)], NN) for s in group]
+        if with_gram:
+            work_out_gram()
+        for s, value in zip(group, values):
+            parts[h, slot(s)] = value
+        if with_gram:
+            send_gram()
+        for s in group:
+            part_copy(h, s).start()
+
+    def scatter_all(h, order):
+        for i in range(0, owners, 4):
+            scatter(h, order[i : i + 4], h == splits - 1 and i == 4)
+
+    @pl.when(is_x)
+    def _():
+        for h in range(splits):
+            if paired:
+                for s in first_collect:
+                    collect(h, s, ())
+            else:
+                each(owners, lambda s: collect(h, s, ()))
+            small[2 * rows * h : 2 * rows * (h + 1)] = stacked(acc[h])
+            if paired:
+                through(second_parts, owners, lambda order: scatter_all(h, order), group=owners)
+            else:
+                each(owners, lambda s: scatter(h, (s,), False))
+        if not paired:
+            work_out_gram()
+            send_gram()
 
         def arrive(s):
             gram_copy(me, lax.rem(me - 1 - s + n, n), 0).wait_recv()
@@ -300,13 +372,22 @@
             total[...] += grams[i + 1]
 
         each(n - 1, add)
-        bottom = total[...]
-        gram = jnp.concatenate([pltpu.roll(bottom, k, axis=1), bottom], axis=0)
+        top = bottom = total[...]
+        if splits == 2:
+            top = jnp.where(lanes < rows, top, pltpu.roll(top, k + rows, axis=1))
+            bottom = jnp.where(lanes < k + rows, pltpu.roll(bottom, rows, axis=1), bottom)
+        gram = jnp.concatenate([pltpu.roll(top, k, axis=1), bottom], axis=0)
         inverse[...] = inverse_factor(gram)
         inverse_copy.start()
 
     @pl.when(is_y)
     def _():
+        for h in range(splits):
+            if paired:
+                for s in second_collect:
+                    collect(h, s, relayed_gathers)
+            else:
+                each(owners, lambda s: collect(h, s, ()))
         inverse_copy.wait_recv()
 
     scale = math.sqrt(width * n)
@@ -358,8 +439,9 @@
                 pltpu.VMEM((n, k // 2, 2 * k), F32),
                 pltpu.VMEM((k // 2, 2 * k), F32),
                 pltpu.VMEM((k, 2 * k), F32),
+                pltpu.VMEM((splits, owners, rows, chunk), F32),
                 dma((owners,)), dma,
-                dma((splits, owners)), dma((splits, n)),
+                dma((splits, owners)), dma((splits, n)), dma((splits, owners)),
                 dma((splits, n)), dma((splits, owners)),
                 dma((n,)), dma((n,)),
                 dma, dma,

time: 35.6 us -> 35.2 us (0.989)
  Pallas kernels: 34.8 us -> 34.4 us
    pallas_call x1, Pallas kernels: 34.8 us -> 34.4 us  [per_device(): pl.pallas_call(functools.partial(kernel, n, owners, chunk, splits), out_s...]
where the time goes in v3:
time: 35.2 us; the launch traced here: 35.1 us
  Pallas kernels  34.4 us (98%)
  local copies, waits for them, and re-layouts  0.66 us (2%)
    pallas_call x1, Pallas kernels, per_device(): pl.pallas_call(functools.partial(kernel, n, owners, chunk, splits), out_s...  34.4 us

profile of v3, /device:TPU:1, one launch (start us, length us, event | category | flops | bytes accessed | tf_op | source)
XLA Modules:
  0.0 35.1 jit_solution(13638172606281894849)
XLA Ops:
  0.0 34.4 %power_pass.1 = f32[1,64,512]{2,1,0:T(8,128)S(1)} custom-call(f32[1,2000,512]{2,1,0:T(8,128)} %data.1, f32[64,512]{1,0:T(8,128)} %sketch.1), custom_call_target="tpu_custom_call" | custom-call | tf_op jit(solution)/shard_map/power_pass/pallas_call | solution.py:422
  34.4 0.7 %copy.4 = f32[1,64,512]{2,1,0:T(8,128)} copy(f32[1,64,512]{2,1,0:T(8,128)S(1)} %power_pass.1) | data formatting | bytes 262144

commit v4 on v3

--- a/solution.py
+++ b/solution.py
@@ -89,7 +89,7 @@
 
 def kernel(
     n, owners, chunk, splits, data, sketch, out, stage, drawn, high, low, high_t, low_t, small, parts, inbox, gathered, acc, grams, total, inverse,
-    passing, load_sem, drawn_sem, part_send, part_recv, pass_recv, gather_send, gather_recv, gram_send, gram_recv, inv_send, inv_recv,
+    load_sem, drawn_sem, part_send, part_recv, gather_send, gather_recv, gram_send, gram_recv, inv_send, inv_recv,
 ):
     me, side = lax.axis_index("cells"), lax.axis_index("side")
     genes, width = data.shape[1:]
@@ -99,20 +99,19 @@
     barrier = pltpu.get_barrier_semaphore()
     paired = owners == n == 8
     loads = first_sends = second_parts = first_gathers = second_gathers = first_collect = second_collect = None
-    relayed_parts = relayed_gathers = ()
+    relayed_gathers = ((),) * splits
     if paired:
         loads = ((5, 4, 7, 6, 2, 1, 3, 0), (7, 6, 5, 1, 3, 2, 4, 0))
         first_sends = (
             (5, 4, 7, 6, 2, 1, 3, 0, 13, 12, 15, 14, 10, 9, 11, 8),
-            (7, 6, 5, 1, 3, 2, 4, 0, 15, 14, 13, 9, 11, 10, 12, 8),
+            (7, 6, 5, 1, 3, 14, 2, 4, 0, 15, 13, 9, 11, 10, 12, 8),
         )
         second_parts = ((5, 4, 7, 6, 2, 3, 1, 0), (6, 1, 5, 4, 3, 2, 7, 0))
-        first_gathers = ((5, 4, 7, 6, 3, 2, 1), (7, 6, 5, 4, 3, 2, 1))
-        second_gathers = ((5, 4, 7, 6, 3, 2, 1), (7, 6, 5, 4, 3, 2, 1))
+        first_gathers = ((5, 4, 7, 6, 2, 3, 1), (7, 5, 6, 4, 3, 2, 1))
+        second_gathers = ((5, 4, 7, 6, 3, 2, 1), (1, 7, 6, 5, 4, 3, 2))
         first_collect = (0, 1, 2, 3, 4, 6, 7, 5)
-        second_collect = (0, 1, 2, 3, 4, 6, 7, 5)
-        relayed_parts = ()
-        relayed_gathers = ()
+        second_collect = (0, 1, 2, 4, 6, 3, 7, 5)
+        relayed_gathers = ((5, 7), ())
 
     def device(cell, which):
         return {"cells": cell, "side": which}
@@ -163,12 +162,6 @@
         ).wait_recv()
         return inbox[h, here]
 
-    def relay_part(h, s):
-        return pltpu.make_async_remote_copy(
-            src_ref=parts.at[h, s], dst_ref=passing.at[h, s - 1], send_sem=part_send.at[h, s],
-            recv_sem=pass_recv.at[h, s - 1], device_id=device(cell_at(1), side), device_id_type=MESH,
-        )
-
     own = 0 if paired else me
 
     def gather_copy(h, s):
@@ -210,21 +203,6 @@
         each(n, lambda s: pl.semaphore_signal(
             barrier, inc=1, device_id=device(lax.rem(me + s, n), 1 - side), device_id_type=MESH
         ))
-
-    if relayed_parts:
-
-        @pl.when(is_y)
-        def _():
-            pl.semaphore_signal(barrier, inc=1, device_id=device(cell_at(1), side), device_id_type=MESH)
-
-    def send_first(h, s):
-        if s in relayed_parts:
-            relay_part(h, s).start()
-            return
-        if s + 1 in relayed_parts:
-            relay_part(h, s + 1).wait_recv()
-            parts[h, s] += passing[h, s]
-        part_copy(h, s).start()
 
     def prepare(s):
         value = stage[slot(s)]
@@ -263,13 +241,13 @@
     def _():
         small[...] = stacked(drawn[...])
         through(loads, owners, prepare_and_work_out, group=4)
-        pl.semaphore_wait(barrier, n + 1 if relayed_parts else n)
+        pl.semaphore_wait(barrier, n)
         if paired:
-            through(first_sends, splits * owners, lambda group: [send_first(*divmod(t, owners)) for t in group])
+            through(first_sends, splits * owners, lambda group: [part_copy(*divmod(t, owners)).start() for t in group])
         else:
             each(owners, lambda s: part_copy(0, s).start())
 
-    def total_up(skipped, order):
+    def total_up(order, relayed):
         for h in range(splits):
 
             def add(s):
@@ -278,19 +256,18 @@
             gathered[h, own] = part_arrival(h, 0)
             if paired:
                 for s in (1, 2, 3, 6, 7, 4, 5):
-                    if s not in skipped:
-                        add(s)
+                    add(s)
             else:
                 each(n - 1, lambda s: add(s + 1))
-            through(order, n, lambda group: [gather_copy(h, s).start() for s in group], 1)
+            through(order, n, lambda group: [gather_copy(h, s).start() for s in group if not paired or s not in relayed[h]], 1)
 
     @pl.when(is_x & (me < owners))
     def _():
-        total_up(relayed_parts, first_gathers)
+        total_up(first_gathers, ((),) * splits)
 
     @pl.when(is_y & (me < owners))
     def _():
-        total_up((), second_gathers)
+        total_up(second_gathers, relayed_gathers)
 
     acc[...] = jnp.zeros_like(acc)
 
@@ -385,7 +362,7 @@
         for h in range(splits):
             if paired:
                 for s in second_collect:
-                    collect(h, s, relayed_gathers)
+                    collect(h, s, relayed_gathers[h])
             else:
                 each(owners, lambda s: collect(h, s, ()))
         inverse_copy.wait_recv()
@@ -439,9 +416,8 @@
                 pltpu.VMEM((n, k // 2, 2 * k), F32),
                 pltpu.VMEM((k // 2, 2 * k), F32),
                 pltpu.VMEM((k, 2 * k), F32),
-                pltpu.VMEM((splits, owners, rows, chunk), F32),
                 dma((owners,)), dma,
-                dma((splits, owners)), dma((splits, n)), dma((splits, owners)),
+                dma((splits, owners)), dma((splits, n)),
                 dma((splits, n)), dma((splits, owners)),
                 dma((n,)), dma((n,)),
                 dma, dma,

time: 35.2 us -> 34 us (0.966)
  Pallas kernels: 34.4 us -> 33.2 us
    pallas_call x1, Pallas kernels: 34.4 us -> 33.2 us  [per_device(): pl.pallas_call(functools.partial(kernel, n, owners, chunk, splits), out_s...]
where the time goes in v4:
time: 34 us; the launch traced here: 33.8 us
  Pallas kernels  33.2 us (98%)
  local copies, waits for them, and re-layouts  0.66 us (2%)
    pallas_call x1, Pallas kernels, per_device(): pl.pallas_call(functools.partial(kernel, n, owners, chunk, splits), out_s...  33.2 us

profile of v4, /device:TPU:1, one launch (start us, length us, event | category | flops | bytes accessed | tf_op | source)
XLA Modules:
  0.0 33.8 jit_solution(7080825973543479190)
XLA Ops:
  0.0 33.2 %power_pass.1 = f32[1,64,512]{2,1,0:T(8,128)S(1)} custom-call(f32[1,2000,512]{2,1,0:T(8,128)} %data.1, f32[64,512]{1,0:T(8,128)} %sketch.1), custom_call_target="tpu_custom_call" | custom-call | tf_op jit(solution)/shard_map/power_pass/pallas_call | solution.py:399
  33.2 0.7 %copy.4 = f32[1,64,512]{2,1,0:T(8,128)} copy(f32[1,64,512]{2,1,0:T(8,128)S(1)} %power_pass.1) | data formatting | bytes 262144

commit v5 on v4

--- a/solution.py
+++ b/solution.py
@@ -194,15 +194,15 @@
         device_id=device(me, 1 - side), device_id_type=MESH,
     )
 
+    @pl.when(is_x)
+    def _():
+        each(n, lambda s: pl.semaphore_signal(
+            barrier, inc=1, device_id=device(lax.rem(me + s, n), 1 - side), device_id_type=MESH
+        ))
+
     draw = pltpu.make_async_copy(sketch, drawn, drawn_sem)
     draw.start()
     through(loads, owners, lambda group: [load(s).start() for s in group])
-
-    @pl.when(is_x)
-    def _():
-        each(n, lambda s: pl.semaphore_signal(
-            barrier, inc=1, device_id=device(lax.rem(me + s, n), 1 - side), device_id_type=MESH
-        ))
 
     def prepare(s):
         value = stage[slot(s)]

time: 34 us -> 34 us (level)
  no operation moved by 1% of the time
where the time goes in v5:
time: 34 us; the launch traced here: 33.8 us
  Pallas kernels  33.2 us (98%)
  local copies, waits for them, and re-layouts  0.66 us (2%)
    pallas_call x1, Pallas kernels, per_device(): pl.pallas_call(functools.partial(kernel, n, owners, chunk, splits), out_s...  33.2 us

profile of v5, /device:TPU:1, one launch (start us, length us, event | category | flops | bytes accessed | tf_op | source)
XLA Modules:
  0.0 33.8 jit_solution(5876708480808938821)
XLA Ops:
  0.0 33.2 %power_pass.1 = f32[1,64,512]{2,1,0:T(8,128)S(1)} custom-call(f32[1,2000,512]{2,1,0:T(8,128)} %data.1, f32[64,512]{1,0:T(8,128)} %sketch.1), custom_call_target="tpu_custom_call" | custom-call | tf_op jit(solution)/shard_map/power_pass/pallas_call | solution.py:399
  33.2 0.7 %copy.4 = f32[1,64,512]{2,1,0:T(8,128)} copy(f32[1,64,512]{2,1,0:T(8,128)S(1)} %power_pass.1) | data formatting | bytes 262144
